TPU v7x, 32 devices: a whole 2x2x4 slice. The times are simulated.
32 devices in a mesh: sx: 4 (over x, core), sy: 4 (over z), dp: 2 (over y).
Axes of the slice: x: 2, y: 2, z: 4, core: 2. Of those that a mesh axis runs over, the one named last changes fastest.
Arguments:
- tokens: bfloat16 [2, 8192, 1280], P('dp', ('sx', 'sy')), may hold values from -6 to 6
- lengths: int32 [2, 64], P('dp'), may hold values from 1 to 512, 8192 in all within a row
- ln_gain: float32 [1280], replicated, may hold values from 0.1 to 1.9
- w_qkv: bfloat16 [1280, 3840], P('dp'), may hold values from -4 to 4, as said below
- w_out: bfloat16 [1280, 1280], P('dp'), may hold values from -0.15625 to 0.15625
Outputs:
- hidden: bfloat16 [2, 8192, 1280], P('dp', ('sx', 'sy'))
- pooled: float32 [2, 64, 1280], P('dp')
Inputs may be any that keep to these rules, and one draw needn't show every extreme that they name: The 64 lengths of a row sum to 8192; images are packed end to end in order. `w_qkv`: columns are queries, then keys, then values, each of 16 heads of 80 columns.
All inputs are finite; a program needn't handle non-finite values.
Results may differ from a plain program's by a relative error of at most 0.0051.
Values may be sent and summed in bfloat16 or wider, within the bound.
A program may use at most 128 MiB of HBM per device.

v0:
```python
import jax
import jax.numpy as jnp
from jax import lax
from jax.sharding import PartitionSpec as P

HEADS = 16
MAXLEN = 512


def with_halo(block, sides, width):
    for axis, dim in sides:
        count = lax.axis_size(axis)
        forward = [(i, i + 1) for i in range(count - 1)]
        backward = [(target, source) for source, target in forward]
        low = lax.ppermute(
            lax.slice_in_dim(block, block.shape[dim] - width, None, axis=dim), axis, forward
        )
        high = lax.ppermute(lax.slice_in_dim(block, 0, width, axis=dim), axis, backward)
        block = jnp.concatenate([low, block, high], axis=dim)
    return block


def image_ids(lengths, positions, total):
    offsets = jnp.cumsum(lengths) - lengths
    counted = jnp.sum((offsets[None, :] <= positions[:, None]).astype(jnp.int32), axis=1) - 1
    inside = (positions >= 0) & (positions < total)
    return jnp.where(inside, counted, -1)


def normalize(rows, ln_gain):
    values = rows.astype(jnp.float32)
    center = values - jnp.mean(values, axis=-1, keepdims=True)
    spread = jnp.mean(center * center, axis=-1, keepdims=True)
    return (center * lax.rsqrt(spread + 1e-05) * ln_gain).astype(jnp.bfloat16)


def attend(queries, keys, values, q_ids, k_ids):
    length = queries.shape[0]
    heads = queries.shape[1]
    block = min(512, length)
    scale = queries.shape[2] ** (-0.5)

    def one_block(index):
        allowed = q_ids[:, None] == k_ids[None, :]

        def one_head(head):
            q_head = lax.dynamic_index_in_dim(queries, head, 1, keepdims=False)
            k_head = lax.dynamic_index_in_dim(keys, head, 1, keepdims=False)
            v_head = lax.dynamic_index_in_dim(values, head, 1, keepdims=False)
            scores = jnp.dot(q_head, k_head.T, preferred_element_type=jnp.float32) * scale
            scores = jnp.where(allowed, scores, -1e30)
            top = jnp.max(scores, axis=1, keepdims=True)
            weights = jnp.exp(scores - top)
            probs = (weights / jnp.sum(weights, axis=1, keepdims=True)).astype(jnp.bfloat16)
            return jnp.dot(probs, v_head, preferred_element_type=jnp.float32).astype(jnp.bfloat16)

        outcome = lax.map(one_head, jnp.arange(heads, dtype=jnp.int32))
        return jnp.transpose(outcome, (1, 0, 2))

    blocks = lax.map(one_block, jnp.arange(length // block, dtype=jnp.int32))
    return blocks.reshape(length, heads, -1)


def shards(tokens, lengths, ln_gain, w_qkv, w_out):
    qkv_full, out_full = (
        lax.all_gather(w_qkv, "dp", axis=0, tiled=True),
        lax.all_gather(w_out, "dp", axis=0, tiled=True),
    )
    count_rows = tokens.shape[0]
    local = tokens.shape[1]
    width = tokens.shape[2]
    size = width // HEADS
    images = lengths.shape[1]
    count_x = lax.axis_size("sx")
    count_y = lax.axis_size("sy")
    total = local * count_x * count_y
    shard = lax.axis_index("sx") * count_y + lax.axis_index("sy")
    own_positions = shard * local + jnp.arange(local, dtype=jnp.int32)
    own_list = [image_ids(lengths[0], own_positions, total)]
    normed = normalize(tokens, ln_gain)
    qkv = jnp.dot(
        normed.reshape(count_rows * local, width), qkv_full, preferred_element_type=jnp.float32
    )
    qkv = qkv.astype(jnp.bfloat16).reshape(count_rows, local, 3 * width)
    pieces = qkv.reshape(count_rows, local, 3, HEADS, size)
    keyvals = with_halo(pieces[:, :, 1:3], ((("sx", "sy"), 1),), MAXLEN)
    k_pos = shard * local - MAXLEN + jnp.arange(local + 2 * MAXLEN, dtype=jnp.int32)
    rowidx = 0
    k_ids = image_ids(lengths[rowidx], k_pos, total)
    outcomes = [
        attend(
            pieces[rowidx, :, 0],
            keyvals[rowidx, :, 0],
            keyvals[rowidx, :, 1],
            own_list[rowidx],
            k_ids,
        )
    ]
    context = jnp.stack(outcomes, axis=0).reshape(count_rows * local, width)
    mixed = jnp.dot(context, out_full, preferred_element_type=jnp.float32).reshape(
        count_rows, local, width
    )
    hidden = (tokens.astype(jnp.float32) + mixed).astype(jnp.bfloat16)
    labels = jnp.arange(images, dtype=jnp.int32)
    rowidx = 0
    onehot = (labels[:, None] == own_list[rowidx][None, :]).astype(jnp.bfloat16)
    parts_list = [jnp.dot(onehot, hidden[rowidx], preferred_element_type=jnp.float32)]
    terms = jnp.stack(parts_list, axis=0)
    sums = lax.psum(terms, ("sx", "sy"))
    pooled = sums / lengths.astype(jnp.float32)[:, :, None]
    return (hidden, pooled)


def solution(mesh):
    in_specs = (P("dp", ("sx", "sy"), None), P("dp", None), P(), P("dp", None), P("dp", None))
    out_specs = (P("dp", ("sx", "sy"), None), P("dp", None, None))
    return jax.shard_map(shards, mesh=mesh, in_specs=in_specs, out_specs=out_specs, check_vma=False)
```

profile of v0, /device:TPU:8, one launch (start us, length us, event | category | flops | bytes accessed | tf_op | source)
XLA Modules:
  0.0 491.2 jit_solution(5797661446178218919)
XLA Ops:
  9.2 123.8 %all-gather.3.cloned.1.call-done = bf16[1280,3840]{1,0:T(8,128)(2,1)} async-done(((bf16[640,3840]{1,0:T(8,128)(2,1)}), bf16[1280,3840]{1,0:T(8,128)(2,1)}) %all-gather.3.cloned.1.call-update) | async-done | bytes 9830416 | tf_op jit(solution)/shard_map/all_gather | solution.py:66
  133.0 10.9 %convolution_convert_fusion = bf16[512,3840]{1,0:T(8,128)(2,1)} fusion(bf16[1280,3840]{1,0:T(8,128)(2,1)} %all-gather.3.cloned.1.call-done, bf16[1,512,1280]{2,1,0:T(8,128)(2,1)S(1)} %copy-done, f32[1280]{0:T(1024)S(1)} %copy-done.4, f32[512]{0:T(512)S(1)} %add_rsqrt_fusion, f32[512]{0:T(512)S(1)} %broadcast_multiply_fusion), kind=kOutput, calls=%fused_computation.19 | convolution fusion | flops 5038407680 | bytes 15082496 | tf_op jit(solution)/shard_map/dot_general | solution.py:81
  144.0 6.3 %copy.10 = bf16[512,3840]{0,1:T(8,128)(2,1)} copy(bf16[512,3840]{1,0:T(8,128)(2,1)} %convolution_convert_fusion) | data formatting | bytes 7864320 | tf_op jit(solution)/shard_map/convert_element_type | solution.py:84
  150.3 1.9 slice.17
  152.2 2.5 collective-permute-start.1
  154.7 3.4 collective-permute-start
  158.7 2.5 slice_bitcast_fusion.2
  161.2 51.9 %collective-permute-done.1 = bf16[1,512,2,16,80]{1,4,3,2,0:T(8,128)(2,1)} collective-permute-done((bf16[1,512,2,16,80]{1,4,3,2,0:T(8,128)(2,1)S(1)}, bf16[1,512,2,16,80]{1,4,3,2,0:T(8,128)(2,1)}, u32[]{:S(2)}, u32[]{:S(2)}) %collective-permute-start.1) | collective-permute-done | bytes 2621472 | tf_op jit(solution)/shard_map/ppermute | solution.py:18
  213.0 28.8 %collective-permute-done = bf16[1,512,2,16,80]{1,4,3,2,0:T(8,128)(2,1)} collective-permute-done((bf16[1,512,2,16,80]{1,4,3,2,0:T(8,128)(2,1)S(1)}, bf16[1,512,2,16,80]{1,4,3,2,0:T(8,128)(2,1)}, u32[]{:S(2)}, u32[]{:S(2)}) %collective-permute-start) | collective-permute-done | bytes 2621472 | tf_op jit(solution)/shard_map/ppermute | solution.py:15
  241.8 3.4 pad_maximum_fusion
  245.3 3.4 slice_bitcast_fusion
  248.6 106.8 %while.18 = (s32[]{:T(128)}, bf16[16,512,80]{1,2,0:T(8,128)(2,1)S(1)}, s32[16]{0:T(128)S(1)}, bf16[512,16,80]{0,2,1:T(8,128)(2,1)}, bf16[1536,16,80]{0,2,1:T(8,1...) while((s32[]{:T(128)}, ...), condition=%wide.region_8.9_spmd.clone, body=%wide.region_5.8_spmd.clone.sunk | while | flops 258776064 | bytes 10112171 | solution.py:57
  253.5 1.8 fusion.40
  260.2 1.8 fusion.40
  266.8 1.8 fusion.40
  273.5 1.8 fusion.40
  280.2 1.8 fusion.40
  286.9 1.8 fusion.40
  293.6 1.8 fusion.40
  300.2 1.8 fusion.40
  306.9 1.8 fusion.40
  313.6 1.8 fusion.40
  320.3 1.8 fusion.40
  326.9 1.8 fusion.40
  333.6 1.8 fusion.40
  340.3 1.8 fusion.40
  347.0 1.8 fusion.40
  351.3 1.8 fusion.38
  353.7 1.8 fusion.40
  356.5 4.2 fusion.18
  361.9 120.9 %all-reduce.2.cloned.1.call-done = f32[1,64,1280]{2,1,0:T(8,128)} async-done(((f32[1,64,1280]{2,1,0:T(8,128)}), f32[1,64,1280]{2,1,0:T(8,128)}) %all-reduce.2.cloned.1.call-update) | async-done | bytes 327696 | tf_op jit(solution)/shard_map/psum | solution.py:109
  482.9 1.8 broadcast_divide_fusion
  (83 shorter events, 49.7 us)
Async XLA Ops:
  7.2 1.3 copy-start
  7.2 125.9 %copy-start.4 = (f32[1280]{0:T(1024)S(1)}, f32[1280]{0:T(1024)}, u32[]{:S(2)}) copy-start(f32[1280]{0:T(1024)} %param.9) | copy-start | bytes 15364
  7.2 125.9 %all-gather.3.cloned.1.call-start = ((), (), s32[]{:S(2)}) async-start(), calls=%async_computation | async-start | bytes 14745600 | tf_op jit(solution)/shard_map/all_gather | solution.py:66
  7.9 347.6 %all-gather.5.cloned.1.call-start = ((), (), s32[]{:S(2)}) async-start(), calls=%async_computation.1 | async-start | bytes 4915200 | tf_op jit(solution)/shard_map/all_gather | solution.py:67
  150.3 7.9 %copy-start.3 = (s32[1,64]{1,0:T(1,128)S(1)}, s32[1,64]{1,0:T(1,128)}, u32[]{:S(2)}) copy-start(s32[1,64]{1,0:T(1,128)} %param.8) | copy-start | bytes 772
  152.2 60.8 %collective-permute-start.1 = (bf16[1,512,2,16,80]{1,4,3,2,0:T(8,128)(2,1)S(1)}, bf16[1,512,2,16,80]{1,4,3,2,0:T(8,128)(2,1)}, u32[]{:S(2)}, u32[]{:S(2)}) collective-permute-start(bf16[1,512,2,16,80]{1,4,3,2,0:T(8,128)(2,1)S(1)} %slice.17), channel_id=1, source_target_pairs={{2,0},{4,2},{6,4},{8,6},{10,8},{12,10},{14,12},{16,14},{18,16},{20... | collective-permute-start | bytes 7864328 | tf_op jit(solution)/shard_map/ppermute | solution.py:18
  154.7 87.1 %collective-permute-start = (bf16[1,512,2,16,80]{1,4,3,2,0:T(8,128)(2,1)S(1)}, bf16[1,512,2,16,80]{1,4,3,2,0:T(8,128)(2,1)}, u32[]{:S(2)}, u32[]{:S(2)}) collective-permute-start(bf16[1,512,2,16,80]{1,4,3,2,0:T(8,128)(2,1)S(1)} %slice.17), channel_id=1, source_target_pairs={{0,2},{2,4},{4,6},{6,8},{8,10},{10,12},{12,14},{14,16},{16,18},{18... | collective-permute-start | bytes 7864328 | tf_op jit(solution)/shard_map/ppermute | solution.py:15
  158.1 324.8 %all-reduce.2.cloned.1.call-start = ((), (), s32[]{:S(2)}) async-start(), calls=%async_computation.2 | async-start | bytes 655360 | tf_op jit(solution)/shard_map/psum | solution.py:109
  245.2 3.4 copy-start.5
  248.6 107.9 %copy-start.1 = (bf16[1,512,1280]{2,1,0:T(8,128)(2,1)S(1)}, bf16[1,512,1280]{2,1,0:T(8,128)(2,1)}, u32[]{:S(2)}) copy-start(bf16[1,512,1280]{2,1,0:T(8,128)(2,1)} %param.7) | copy-start | bytes 3932164
  355.5 1.1 copy-start.6
  360.8 123.9 %copy-start.2 = (bf16[1,512,1280]{2,1,0:T(8,128)(2,1)}, bf16[1,512,1280]{2,1,0:T(8,128)(2,1)S(1)}, u32[]{:S(2)}) copy-start(bf16[1,512,1280]{2,1,0:T(8,128)(2,1)S(1)} %fusion.18) | copy-start | bytes 3932164
Sparse Core Ops, SparseCore 0:
  9.6 123.4 all-gather.2
  158.2 47.8 all-gather.4
  362.1 120.7 all-reduce.1
where the time goes:
time: 493 us; the launch traced here: 491 us
  waiting for transfers between devices  326 us (66%)
  matrix products  73.3 us (15%)
  loops' own time  31.3 us (6%)
  local copies, waits for them, and re-layouts  25 us (5%)
  other arithmetic  15.6 us (3%)
  between operations  13.9 us (3%)
  starting transfers between devices  5.96 us (1%)
    all_gather x1, waiting for transfers between devices, shards(): lax.all_gather(w_qkv, 'dp', axis=0, tiled=True)  124 us
    psum x1, waiting for transfers between devices, shards(): sums = lax.psum(terms, ('sx', 'sy'))  121 us
    ppermute x1, waiting for transfers between devices, with_halo(): lax.ppermute(lax.slice_in_dim(block, 0, width, axis=dim), axis, backward)  51.9 us
    another operation x1, loops' own time, one_block(): outcome = lax.map(one_head, jnp.arange(heads, dtype=jnp.int32))  31.3 us
    dot_general x16, matrix products, one_head(): jnp.dot(probs, v_head, preferred_element_type=jnp.float32)  28.9 us
    ppermute x1, waiting for transfers between devices, with_halo(): lax.ppermute(lax.slice_in_dim(block, block.shape[dim] - width, None, axis...  28.8 us
    dot_general x16, matrix products, one_head(): jnp.dot(q_head, k_head.T, preferred_element_type=jnp.float32) * scale  28.1 us
    dot_general x1, matrix products, shards(): jnp.dot(normed.reshape(count_rows * local, width), qkv_full, preferred_el...  10.9 us
  transfers between devices with their start and end apart: 5, of which 4 were waited for; matrix products, arithmetic and copies ran while one was open for 18% of the time, Pallas kernels for 0%

commit v1 on v0

--- a/solution.py
+++ b/solution.py
@@ -5,6 +5,12 @@
 
 HEADS = 16
 MAXLEN = 512
+
+
+def change_table(w_in, net_axis, a_name):
+    for p in (net_axis, a_name):
+        w_in = lax.psum(w_in, p)
+    return w_in
 
 
 def with_halo(block, sides, width):
@@ -106,7 +112,7 @@
     onehot = (labels[:, None] == own_list[rowidx][None, :]).astype(jnp.bfloat16)
     parts_list = [jnp.dot(onehot, hidden[rowidx], preferred_element_type=jnp.float32)]
     terms = jnp.stack(parts_list, axis=0)
-    sums = lax.psum(terms, ("sx", "sy"))
+    sums = change_table(terms, "sx", "sy")
     pooled = sums / lengths.astype(jnp.float32)[:, :, None]
     return (hidden, pooled)
 

time: 493 us -> 474 us (0.961)
  waiting for transfers between devices: 326 us -> 306 us
    psum x1 -> x2, waiting for transfers between devices: 121 us -> 101 us  [change_table(): w_in = lax.psum(w_in, p)]
  transfers between devices with their start and end apart: 5 -> 6, of which waited for: 4 -> 5; matrix products, arithmetic and copies ran while one was open for 18% -> 18% of each run, Pallas kernels for 0% -> 0%
where the time goes in v1:
time: 474 us; the launch traced here: 471 us
  waiting for transfers between devices  306 us (65%)
  matrix products  73.3 us (15%)
  loops' own time  31.3 us (7%)
  local copies, waits for them, and re-layouts  25 us (5%)
  other arithmetic  15.6 us (3%)
  between operations  13.9 us (3%)
  starting transfers between devices  6 us (1%)
    all_gather x1, waiting for transfers between devices, shards(): lax.all_gather(w_qkv, 'dp', axis=0, tiled=True)  124 us
    psum x2, waiting for transfers between devices, change_table(): w_in = lax.psum(w_in, p)  101 us
    ppermute x1, waiting for transfers between devices, with_halo(): lax.ppermute(lax.slice_in_dim(block, 0, width, axis=dim), axis, backward)  51.9 us
    another operation x1, loops' own time, one_block(): outcome = lax.map(one_head, jnp.arange(heads, dtype=jnp.int32))  31.3 us
    dot_general x16, matrix products, one_head(): jnp.dot(probs, v_head, preferred_element_type=jnp.float32)  28.9 us
    ppermute x1, waiting for transfers between devices, with_halo(): lax.ppermute(lax.slice_in_dim(block, block.shape[dim] - width, None, axis...  28.8 us
    dot_general x16, matrix products, one_head(): jnp.dot(q_head, k_head.T, preferred_element_type=jnp.float32) * scale  28.1 us
    dot_general x1, matrix products, shards(): jnp.dot(normed.reshape(count_rows * local, width), qkv_full, preferred_el...  10.9 us
  transfers between devices with their start and end apart: 6, of which 5 were waited for; matrix products, arithmetic and copies ran while one was open for 18% of the time, Pallas kernels for 0%

profile of v1, /device:TPU:8, one launch (start us, length us, event | category | flops | bytes accessed | tf_op | source)
XLA Modules:
  0.0 471.2 jit_solution(6965288757414528228)
XLA Ops:
  9.2 123.8 %all-gather.3.cloned.1.call-done = bf16[1280,3840]{1,0:T(8,128)(2,1)} async-done(((bf16[640,3840]{1,0:T(8,128)(2,1)}), bf16[1280,3840]{1,0:T(8,128)(2,1)}) %all-gather.3.cloned.1.call-update) | async-done | bytes 9830416 | tf_op jit(solution)/shard_map/all_gather | solution.py:72
  133.0 10.9 %convolution_convert_fusion = bf16[512,3840]{1,0:T(8,128)(2,1)} fusion(bf16[1280,3840]{1,0:T(8,128)(2,1)} %all-gather.3.cloned.1.call-done, bf16[1,512,1280]{2,1,0:T(8,128)(2,1)S(1)} %copy-done, f32[1280]{0:T(1024)S(1)} %copy-done.4, f32[512]{0:T(512)S(1)} %add_rsqrt_fusion, f32[512]{0:T(512)S(1)} %broadcast_multiply_fusion), kind=kOutput, calls=%fused_computation.19 | convolution fusion | flops 5038407680 | bytes 15082496 | tf_op jit(solution)/shard_map/dot_general | solution.py:87
  144.0 6.3 %copy.10 = bf16[512,3840]{0,1:T(8,128)(2,1)} copy(bf16[512,3840]{1,0:T(8,128)(2,1)} %convolution_convert_fusion) | data formatting | bytes 7864320 | tf_op jit(solution)/shard_map/convert_element_type | solution.py:90
  150.3 1.9 slice.17
  152.2 2.5 collective-permute-start.1
  154.7 3.4 collective-permute-start
  158.7 2.5 slice_bitcast_fusion.2
  161.2 51.9 %collective-permute-done.1 = bf16[1,512,2,16,80]{1,4,3,2,0:T(8,128)(2,1)} collective-permute-done((bf16[1,512,2,16,80]{1,4,3,2,0:T(8,128)(2,1)S(1)}, bf16[1,512,2,16,80]{1,4,3,2,0:T(8,128)(2,1)}, u32[]{:S(2)}, u32[]{:S(2)}) %collective-permute-start.1) | collective-permute-done | bytes 2621472 | tf_op jit(solution)/shard_map/ppermute | solution.py:24
  213.0 28.8 %collective-permute-done = bf16[1,512,2,16,80]{1,4,3,2,0:T(8,128)(2,1)} collective-permute-done((bf16[1,512,2,16,80]{1,4,3,2,0:T(8,128)(2,1)S(1)}, bf16[1,512,2,16,80]{1,4,3,2,0:T(8,128)(2,1)}, u32[]{:S(2)}, u32[]{:S(2)}) %collective-permute-start) | collective-permute-done | bytes 2621472 | tf_op jit(solution)/shard_map/ppermute | solution.py:21
  241.8 3.4 pad_maximum_fusion
  245.3 3.4 slice_bitcast_fusion
  248.6 106.8 %while.18 = (s32[]{:T(128)}, bf16[16,512,80]{1,2,0:T(8,128)(2,1)S(1)}, s32[16]{0:T(128)S(1)}, bf16[512,16,80]{0,2,1:T(8,128)(2,1)}, bf16[1536,16,80]{0,2,1:T(8,1...) while((s32[]{:T(128)}, ...), condition=%wide.region_8.9_spmd.clone, body=%wide.region_5.8_spmd.clone.sunk | while | flops 258776064 | bytes 10112171 | solution.py:63
  253.5 1.8 fusion.40
  260.2 1.8 fusion.40
  266.8 1.8 fusion.40
  273.5 1.8 fusion.40
  280.2 1.8 fusion.40
  286.9 1.8 fusion.40
  293.6 1.8 fusion.40
  300.2 1.8 fusion.40
  306.9 1.8 fusion.40
  313.6 1.8 fusion.40
  320.3 1.8 fusion.40
  326.9 1.8 fusion.40
  333.6 1.8 fusion.40
  340.3 1.8 fusion.40
  347.0 1.8 fusion.40
  353.7 1.8 fusion.40
  356.5 4.2 fusion.18
  362.0 62.1 %all-reduce.3.cloned.1.call-done = f32[1,64,1280]{2,1,0:T(8,128)} async-done(((f32[1,64,1280]{2,1,0:T(8,128)}), f32[1,64,1280]{2,1,0:T(8,128)}) %all-reduce.3.cloned.1.call-update) | async-done | bytes 327696 | tf_op jit(solution)/shard_map/psum | solution.py:12
  424.2 38.7 %all-reduce.5.cloned.1.call-done = f32[1,64,1280]{2,1,0:T(8,128)} async-done(((f32[1,64,1280]{2,1,0:T(8,128)}), f32[1,64,1280]{2,1,0:T(8,128)}) %all-reduce.5.cloned.1.call-update) | async-done | bytes 327696 | tf_op jit(solution)/shard_map/psum | solution.py:12
  462.8 1.8 broadcast_divide_fusion
  (86 shorter events, 51.5 us)
Async XLA Ops:
  7.2 1.3 copy-start
  7.2 125.9 %copy-start.4 = (f32[1280]{0:T(1024)S(1)}, f32[1280]{0:T(1024)}, u32[]{:S(2)}) copy-start(f32[1280]{0:T(1024)} %param.9) | copy-start | bytes 15364
  7.2 125.9 %all-gather.3.cloned.1.call-start = ((), (), s32[]{:S(2)}) async-start(), calls=%async_computation | async-start | bytes 14745600 | tf_op jit(solution)/shard_map/all_gather | solution.py:72
  7.9 347.6 %all-gather.5.cloned.1.call-start = ((), (), s32[]{:S(2)}) async-start(), calls=%async_computation.1 | async-start | bytes 4915200 | tf_op jit(solution)/shard_map/all_gather | solution.py:73
  150.3 7.9 %copy-start.3 = (s32[1,64]{1,0:T(1,128)S(1)}, s32[1,64]{1,0:T(1,128)}, u32[]{:S(2)}) copy-start(s32[1,64]{1,0:T(1,128)} %param.8) | copy-start | bytes 772
  152.2 60.8 %collective-permute-start.1 = (bf16[1,512,2,16,80]{1,4,3,2,0:T(8,128)(2,1)S(1)}, bf16[1,512,2,16,80]{1,4,3,2,0:T(8,128)(2,1)}, u32[]{:S(2)}, u32[]{:S(2)}) collective-permute-start(bf16[1,512,2,16,80]{1,4,3,2,0:T(8,128)(2,1)S(1)} %slice.17), channel_id=1, source_target_pairs={{2,0},{4,2},{6,4},{8,6},{10,8},{12,10},{14,12},{16,14},{18,16},{20... | collective-permute-start | bytes 7864328 | tf_op jit(solution)/shard_map/ppermute | solution.py:24
  154.7 87.1 %collective-permute-start = (bf16[1,512,2,16,80]{1,4,3,2,0:T(8,128)(2,1)S(1)}, bf16[1,512,2,16,80]{1,4,3,2,0:T(8,128)(2,1)}, u32[]{:S(2)}, u32[]{:S(2)}) collective-permute-start(bf16[1,512,2,16,80]{1,4,3,2,0:T(8,128)(2,1)S(1)} %slice.17), channel_id=1, source_target_pairs={{0,2},{2,4},{4,6},{6,8},{8,10},{10,12},{12,14},{14,16},{16,18},{18... | collective-permute-start | bytes 7864328 | tf_op jit(solution)/shard_map/ppermute | solution.py:21
  158.1 266.0 %all-reduce.3.cloned.1.call-start = ((), (), s32[]{:S(2)}) async-start(), calls=%async_computation.2 | async-start | bytes 655360 | tf_op jit(solution)/shard_map/psum | solution.py:12
  245.2 3.4 copy-start.5
  248.6 107.9 %copy-start.1 = (bf16[1,512,1280]{2,1,0:T(8,128)(2,1)S(1)}, bf16[1,512,1280]{2,1,0:T(8,128)(2,1)}, u32[]{:S(2)}) copy-start(bf16[1,512,1280]{2,1,0:T(8,128)(2,1)} %param.7) | copy-start | bytes 3932164
  355.5 1.1 copy-start.6
  360.8 103.9 %copy-start.2 = (bf16[1,512,1280]{2,1,0:T(8,128)(2,1)}, bf16[1,512,1280]{2,1,0:T(8,128)(2,1)S(1)}, u32[]{:S(2)}) copy-start(bf16[1,512,1280]{2,1,0:T(8,128)(2,1)S(1)} %fusion.18) | copy-start | bytes 3932164
  361.9 100.9 %all-reduce.5.cloned.1.call-start = ((), (), s32[]{:S(2)}) async-start(), calls=%async_computation.3 | async-start | bytes 655360 | tf_op jit(solution)/shard_map/psum | solution.py:12
Sparse Core Ops, SparseCore 0:
  9.6 123.4 all-gather.2
  158.2 47.8 all-gather.4
  362.1 62.0 all-reduce.2
  426.3 36.4 all-reduce.4
